TPU v7x, 32 devices: a whole 2x2x4 slice. The times are simulated.
32 devices in a mesh: rows: 8 (over z, x), cols: 4 (over y, core).
Axes of the slice: x: 2, y: 2, z: 4, core: 2. Of those that a mesh axis runs over, the one named last changes fastest.
Arguments:
- vectors: bfloat16 [1024, 32768], P(None, 'rows'), may hold values from -0.4 to 0.4
- integrals: bfloat16 [2, 256, 32768], P(None, 'cols', 'rows'), may hold values from -8 to 72
- pivots: int32 [2, 256], replicated, may hold values from 0 to 32767, as said below
Outputs:
- new_vectors: float32 [2, 256, 32768], P(None, 'cols', 'rows')
Inputs may be any that keep to these rules, and one draw needn't show every extreme that they name: The 2 x 256 entries are distinct shell-pair rows. In each panel the rows of one index of rows (an aligned block of 4096) hold at most 64 pivots, and some block holds exactly 64.
All inputs are finite; a program needn't handle non-finite values.
Results may differ from a plain program's by a relative error of at most 0.00036.
Values may be sent and summed in bfloat16 or wider, within the bound.
No kernel may reach another device: no remote copies, remote signals or barrier semaphores. Data moves between devices by JAX's collectives and lax.ppermute only.
A program may use at most 64 MiB of HBM per device.

v0:
```python
import jax
import jax.numpy as jnp
from jax import lax
from jax.sharding import PartitionSpec as P

PW = 256
PANELS = 2


def select_matrix(row_count, targets):
    return (jnp.arange(row_count, dtype=jnp.int32)[:, None] == targets[None, :]).astype(
        jnp.bfloat16
    )


def transposed_product(left, right):
    return lax.dot_general(
        left, right, (((0,), (0,)), ((), ())), preferred_element_type=jnp.float32
    )


def solve_block(lower_factor, residual):
    return jax.scipy.linalg.solve_triangular(lower_factor, residual, lower=True)


def per_device(vectors, integrals, pivots):
    row_count = vectors.shape[1]
    block_cols = integrals.shape[1]
    owners = lax.axis_size("rows")
    owner_index = lax.axis_index("rows")
    owner_start = owner_index * row_count
    col_start = lax.axis_index("cols") * block_cols
    factors = [vectors]
    results = []
    for panel in range(PANELS):
        pivot_row = pivots[panel]
        local_targets = pivot_row - owner_start
        slot_count = 2 * PW // owners
        owner_of = pivot_row // row_count
        order = jnp.arange(PW, dtype=jnp.int32)
        earlier = (owner_of[None, :] == owner_of[:, None]) & (order[None, :] < order[:, None])
        slot_rank = jnp.sum(earlier.astype(jnp.int32), axis=1)
        mine = owner_of == owner_index
        slot_pick = (
            (slot_rank[:, None] == jnp.arange(slot_count, dtype=jnp.int32)[None, :]) & mine[:, None]
        ).astype(jnp.bfloat16)
        slot_select = jnp.dot(
            select_matrix(row_count, local_targets), slot_pick, preferred_element_type=jnp.float32
        ).astype(jnp.bfloat16)
        sending = jnp.concatenate(
            [
                jnp.dot(factor, slot_select, preferred_element_type=jnp.float32)
                for factor in factors
            ],
            axis=0,
        ).astype(jnp.bfloat16)
        targets = lax.dynamic_slice_in_dim(owner_of * slot_count + slot_rank, col_start, block_cols)
        receive_pick = select_matrix(owners * slot_count, targets)
        picked = jnp.dot(
            lax.all_gather(sending, "rows", axis=1, tiled=True),
            receive_pick,
            preferred_element_type=jnp.float32,
        ).astype(jnp.bfloat16)
        residual = integrals[panel].astype(jnp.float32)
        offset = 0
        for factor in factors:
            residual = residual - transposed_product(
                picked[offset : offset + factor.shape[0]], factor
            )
            offset = offset + factor.shape[0]
        every_pivot = select_matrix(row_count, local_targets).astype(jnp.float32)
        contribution = jnp.dot(residual, every_pivot, precision=lax.Precision.HIGHEST)
        placed = lax.dynamic_update_slice(
            jnp.zeros((PW, PW), jnp.float32), contribution, (col_start, 0)
        )
        block = lax.psum(placed, ("rows", "cols"))
        lower_factor = jnp.linalg.cholesky(0.5 * (block + block.T))
        whole = lax.all_gather(residual, "cols", axis=0, tiled=True)
        solved = solve_block(lower_factor, whole)
        fresh = lax.dynamic_slice_in_dim(solved, col_start, block_cols, 0)
        if panel + 1 < PANELS:
            factors.append(solved.astype(jnp.bfloat16))
        results.append(fresh)
    return jnp.stack(results)


def solution(mesh):
    placed = (P(None, "rows"), P(None, "cols", "rows"), P())
    return jax.shard_map(
        per_device, mesh=mesh, in_specs=placed, out_specs=P(None, "cols", "rows"), check_vma=False
    )
```

profile of v0, /device:TPU:0, one launch (start us, length us, event | category | flops | bytes accessed | tf_op | source)
XLA Modules:
  0.0 519.9 jit_solution(4560592978291593466)
XLA Ops:
  6.5 0.8 fusion.58
  7.5 7.5 %fusion.14 = bf16[1024,64]{0,1:T(8,128)(2,1)} fusion(bf16[1024,4096]{1,0:T(8,128)(2,1)} %param.6, s32[256]{0:T(256)S(1)} %bitcast.98, s32[256]{0:T(256)S(1)} %convert_reduce_fusion.1, pred[256]{0:T(512)(128)(4,1)S(1)} %get-tuple-element.65), kind=kOutput, calls=%fused_computation.36 | convolution fusion | flops 672497664 | bytes 8521984 | tf_op jit(solution)/shard_map/dot_general | solution.py:52
  15.2 43.0 %all-gather.5.cloned.1.call-done = bf16[1024,512]{0,1:T(8,128)(2,1)} async-done(((bf16[1024,64]{0,1:T(8,128)(2,1)}), bf16[1024,512]{0,1:T(8,128)(2,1)}) %all-gather.5.cloned.1.call-update) | async-done | bytes 1048592 | tf_op jit(solution)/shard_map/all_gather | solution.py:60
  58.2 5.9 %convolution_subtract_fusion.4 = f32[64,4096]{1,0:T(8,128)S(1)} fusion(bf16[1024,4096]{1,0:T(8,128)(2,1)} %param.6, bf16[1024,512]{0,1:T(8,128)(2,1)} %all-gather.5.cloned.1.call-done, bf16[2,64,4096]{2,1,0:T(8,128)(2,1)S(1)} %copy-done.6, s32[64]{0:T(128)S(1)} %dynamic_slice.12), kind=kOutput, calls=%fused_computation.12 | convolution fusion | flops 604602368 | bytes 11010304 | tf_op jit(solution)/shard_map/dot_general | solution.py:17
  64.1 1.7 fusion.15
  65.8 0.7 copy-done.8
  66.6 0.7 all-gather.7.cloned.1.call-update
  67.7 1.0 convolution_convert_fusion.1
  68.7 6.1 %fusion.13 = bf16[1024,64]{0,1:T(8,128)(2,1)S(1)} fusion(bf16[4096,64]{0,1:T(8,128)(2,1)S(1)} %convolution_convert_fusion.1, bf16[1024,4096]{1,0:T(8,128)(2,1)} %param.6), kind=kOutput, calls=%fused_computation.35 | convolution fusion | flops 536936448 | bytes 9043968 | tf_op jit(solution)/shard_map/dot_general | solution.py:52
  74.7 117.2 %all-reduce.4.cloned.1.call-done = f32[256,256]{1,0:T(8,128)} async-done(((f32[256,256]{1,0:T(8,128)}), f32[256,256]{1,0:T(8,128)}) %all-reduce.4.cloned.1.call-update) | async-done | bytes 262160 | tf_op jit(solution)/shard_map/psum | solution.py:76
  192.0 1.1 copy.9
  193.1 1.0 fusion.25
  194.2 11.7 %cholesky.130 = f32[128,128]{1,0:T(8,128)S(1)} custom-call(f32[128,128]{1,0:T(8,128)S(1)} %cholesky.194), custom_call_target="Cholesky" | custom-call | tf_op jit(solution)/shard_map/jit(cholesky)/cholesky | solution.py:77
  206.0 9.8 %custom-call.13 = f32[1,128,128]{1,2,0:T(8,128)S(1)} custom-call(f32[1,128,128]{2,1,0:T(8,128)S(1)} %get-tuple-element.54), custom_call_target="InvertDiagBlocksLowerTriangular" | custom-call | tf_op jit(solution)/shard_map/jit(cholesky)/cholesky | solution.py:77
  216.3 11.9 %cholesky.147 = f32[128,128]{1,0:T(8,128)S(1)} custom-call(f32[128,128]{1,0:T(8,128)S(1)} %convolution_subtract_fusion.6), custom_call_target="Cholesky" | custom-call | tf_op jit(solution)/shard_map/jit(cholesky)/cholesky | solution.py:77
  228.2 0.7 compare_reduce_fusion.3
  228.9 0.7 compare_reduce_fusion.2
  231.0 4.1 while.4
  231.0 0.6 fusion.79
  231.7 1.4 bitcast_dynamic-update-slice_fusion.4
  233.1 0.6 fusion.79
  233.7 1.4 bitcast_dynamic-update-slice_fusion.4
  235.1 19.7 %custom-call.14 = f32[2,128,128]{1,2,0:T(8,128)S(1)} custom-call(f32[2,128,128]{2,1,0:T(8,128)S(1)} %get-tuple-element.21), custom_call_target="InvertDiagBlocksLowerTriangular" | custom-call | tf_op jit(solution)/shard_map/jit(_solve_triangular)/triangular_solve | solution.py:23
  254.8 3.6 fusion.5
  258.5 1.9 convolution_subtract_fusion.1
  260.4 1.9 fusion.42
  262.4 0.8 convolution_convert_fusion.5
  263.7 0.7 pad_maximum_fusion.2
  264.6 40.9 %all-gather.9.cloned.1.call-done = bf16[1280,512]{0,1:T(8,128)(2,1)} async-done(((bf16[1280,64]{0,1:T(8,128)(2,1)}), bf16[1280,512]{0,1:T(8,128)(2,1)}) %all-gather.9.cloned.1.call-update) | async-done | bytes 1310736 | tf_op jit(solution)/shard_map/all_gather | solution.py:60
  305.5 1.7 convolution_convert_fusion.2
  307.2 5.1 convolution_subtract_fusion.3
  312.9 1.7 fusion.16
  314.6 0.7 copy-done.9
  316.0 124.8 %all-reduce.6.cloned.1.call-done = f32[256,256]{1,0:T(8,128)} async-done(((f32[256,256]{1,0:T(8,128)}), f32[256,256]{1,0:T(8,128)}) %all-reduce.6.cloned.1.call-update) | async-done | bytes 262160 | tf_op jit(solution)/shard_map/psum | solution.py:76
  440.9 1.1 copy.11
  441.9 1.0 bitcast_add_fusion.1
  443.3 11.7 %cholesky.164 = f32[128,128]{1,0:T(8,128)S(1)} custom-call(f32[128,128]{1,0:T(8,128)S(1)} %cholesky.197), custom_call_target="Cholesky" | custom-call | tf_op jit(solution)/shard_map/jit(cholesky)/cholesky | solution.py:77
  455.0 9.8 %custom-call.15 = f32[1,128,128]{1,2,0:T(8,128)S(1)} custom-call(f32[1,128,128]{2,1,0:T(8,128)S(1)} %get-tuple-element.50), custom_call_target="InvertDiagBlocksLowerTriangular" | custom-call | tf_op jit(solution)/shard_map/jit(cholesky)/cholesky | solution.py:77
  465.4 11.7 %cholesky.181 = f32[128,128]{1,0:T(8,128)S(1)} custom-call(f32[128,128]{1,0:T(8,128)S(1)} %convolution_subtract_fusion.5), custom_call_target="Cholesky" | custom-call | tf_op jit(solution)/shard_map/jit(cholesky)/cholesky | solution.py:77
  477.8 0.6 compare_reduce_fusion
  479.7 4.1 while.5
  480.5 1.4 bitcast_dynamic-update-slice_fusion.5
  482.5 1.4 bitcast_dynamic-update-slice_fusion.5
  483.9 19.7 %custom-call.16 = f32[2,128,128]{1,2,0:T(8,128)S(1)} custom-call(f32[2,128,128]{2,1,0:T(8,128)S(1)} %get-tuple-element.22), custom_call_target="InvertDiagBlocksLowerTriangular" | custom-call | tf_op jit(solution)/shard_map/jit(_solve_triangular)/triangular_solve | solution.py:23
  503.6 3.6 fusion.3
  507.2 1.9 convolution_subtract_fusion
  509.2 1.9 fusion.38
  511.3 1.5 pad_maximum_fusion.1
  (74 shorter events, 6.6 us)
Async XLA Ops:
  6.5 51.7 %all-gather.5.cloned.1.call-start = ((), (), s32[]{:S(2)}) async-start(), calls=%async_computation | async-start | bytes 1179648 | tf_op jit(solution)/shard_map/all_gather | solution.py:60
  7.5 50.7 %copy-start.6 = (bf16[2,64,4096]{2,1,0:T(8,128)(2,1)S(1)}, bf16[2,64,4096]{2,1,0:T(8,128)(2,1)}, u32[]{:S(2)}) copy-start(bf16[2,64,4096]{2,1,0:T(8,128)(2,1)} %param.7) | copy-start | bytes 3145732
  15.0 176.9 %all-reduce.4.cloned.1.call-start = ((), (), s32[]{:S(2)}) async-start(), calls=%async_computation.1 | async-start | bytes 524288 | tf_op jit(solution)/shard_map/psum | solution.py:76
  64.1 2.5 copy-start.5
  65.8 0.7 copy-start.8
  66.5 188.3 %all-gather.7.cloned.1.call-start = ((), (), s32[]{:S(2)}) async-start(), calls=%async_computation.2 | async-start | bytes 5242880 | tf_op jit(solution)/shard_map/all_gather | solution.py:78
  67.3 238.2 %all-gather.9.cloned.1.call-start = ((), (), s32[]{:S(2)}) async-start(), calls=%async_computation.3 | async-start | bytes 1474560 | tf_op jit(solution)/shard_map/all_gather | solution.py:60
  254.8 3.7 copy-start.2
  262.4 1.3 copy-start
  263.7 43.5 %copy-start.7 = (bf16[2,64,4096]{2,1,0:T(8,128)(2,1)S(1)}, bf16[2,64,4096]{2,1,0:T(8,128)(2,1)}, u32[]{:S(2)}) copy-start(bf16[2,64,4096]{2,1,0:T(8,128)(2,1)} %param.7) | copy-start | bytes 3145732
  264.4 176.4 %all-reduce.6.cloned.1.call-start = ((), (), s32[]{:S(2)}) async-start(), calls=%async_computation.4 | async-start | bytes 524288 | tf_op jit(solution)/shard_map/psum | solution.py:76
  307.2 5.2 copy-start.1
  312.9 2.9 copy-start.4
  314.6 0.7 copy-start.9
  315.3 188.3 %all-gather.11.cloned.1.call-start = ((), (), s32[]{:S(2)}) async-start(), calls=%async_computation.5 | async-start | bytes 5242880 | tf_op jit(solution)/shard_map/all_gather | solution.py:78
  503.6 3.7 copy-start.3
Sparse Core Ops, SparseCore 0:
  15.2 42.9 all-gather.4
  66.6 125.2 all-reduce.3
  193.5 33.7 all-gather.6
  264.5 40.8 all-gather.8
  315.4 125.3 all-reduce.5
  442.3 33.6 all-gather.10
where the time goes:
time: 525 us; the launch traced here: 520 us
  waiting for transfers between devices  327 us (62%)
  other arithmetic  115 us (22%)
  matrix products  47.8 us (9%)
  between operations  16.7 us (3%)
  local copies, waits for them, and re-layouts  12.8 us (2%)
    psum x2, waiting for transfers between devices, per_device(): block = lax.psum(placed, ('rows', 'cols'))  242 us
    all_gather x2, waiting for transfers between devices, per_device(): lax.all_gather(sending, 'rows', axis=1, tiled=True)  83.9 us
    another operation x14, other arithmetic, per_device(): lower_factor = jnp.linalg.cholesky(0.5 * (block + block.T))  69.4 us
    another operation x5, other arithmetic, solve_block(): return jax.scipy.linalg.solve_triangular(lower_factor, residual, lower=True)  39.4 us
    another operation x6, matrix products, solve_block(): return jax.scipy.linalg.solve_triangular(lower_factor, residual, lower=True)  15 us
    dot_general x3, matrix products, per_device(): jnp.dot(factor, slot_select, preferred_element_type=jnp.float32)  14.4 us
    dot_general x3, matrix products, transposed_product(): lax.dot_general(left, right, (((0,), (0,)), ((), ())), preferred_element_...  11.5 us
  transfers between devices with their start and end apart: 6, of which 4 were waited for; matrix products, arithmetic and copies ran while one was open for 25% of the time, Pallas kernels for 0%

commit v1 on v0

--- a/solution.py
+++ b/solution.py
@@ -73,7 +73,8 @@
         placed = lax.dynamic_update_slice(
             jnp.zeros((PW, PW), jnp.float32), contribution, (col_start, 0)
         )
-        block = lax.psum(placed, ("rows", "cols"))
+        half = lax.psum(placed, "cols")
+        block = lax.psum(half, "rows")
         lower_factor = jnp.linalg.cholesky(0.5 * (block + block.T))
         whole = lax.all_gather(residual, "cols", axis=0, tiled=True)
         solved = solve_block(lower_factor, whole)

time: 525 us -> 486 us (0.926)
  waiting for transfers between devices: 327 us -> 287 us
    psum x2 -> x4, waiting for transfers between devices: 242 us -> 202 us  [the longest x2 140 us: per_device(): block = lax.psum(half, 'rows')]
  transfers between devices with their start and end apart: 6 -> 8, of which waited for: 4 -> 6; matrix products, arithmetic and copies ran while one was open for 25% -> 27% of each run, Pallas kernels for 0% -> 0%
where the time goes in v1:
time: 486 us; the launch traced here: 480 us
  waiting for transfers between devices  287 us (59%)
  other arithmetic  115 us (24%)
  matrix products  47.8 us (10%)
  between operations  16.7 us (3%)
  local copies, waits for them, and re-layouts  12.8 us (3%)
    psum x2, waiting for transfers between devices, per_device(): block = lax.psum(half, 'rows')  140 us
    all_gather x2, waiting for transfers between devices, per_device(): lax.all_gather(sending, 'rows', axis=1, tiled=True)  84 us
    another operation x14, other arithmetic, per_device(): lower_factor = jnp.linalg.cholesky(0.5 * (block + block.T))  69.5 us
    psum x2, waiting for transfers between devices, per_device(): half = lax.psum(placed, 'cols')  62.3 us
    another operation x5, other arithmetic, solve_block(): return jax.scipy.linalg.solve_triangular(lower_factor, residual, lower=True)  39.4 us
    another operation x6, matrix products, solve_block(): return jax.scipy.linalg.solve_triangular(lower_factor, residual, lower=True)  15 us
    dot_general x3, matrix products, per_device(): jnp.dot(factor, slot_select, preferred_element_type=jnp.float32)  14.3 us
    dot_general x3, matrix products, transposed_product(): lax.dot_general(left, right, (((0,), (0,)), ((), ())), preferred_element_...  11.5 us
  transfers between devices with their start and end apart: 8, of which 6 were waited for; matrix products, arithmetic and copies ran while one was open for 27% of the time, Pallas kernels for 0%

profile of v1, /device:TPU:0, one launch (start us, length us, event | category | flops | bytes accessed | tf_op | source)
XLA Modules:
  0.0 480.3 jit_solution(2782597846670198541)
XLA Ops:
  6.5 0.8 fusion.58
  7.5 7.5 %fusion.14 = bf16[1024,64]{0,1:T(8,128)(2,1)} fusion(bf16[1024,4096]{1,0:T(8,128)(2,1)} %param.6, s32[256]{0:T(256)S(1)} %bitcast.98, s32[256]{0:T(256)S(1)} %convert_reduce_fusion.1, pred[256]{0:T(512)(128)(4,1)S(1)} %get-tuple-element.65), kind=kOutput, calls=%fused_computation.36 | convolution fusion | flops 672497664 | bytes 8521984 | tf_op jit(solution)/shard_map/dot_general | solution.py:52
  15.2 43.0 %all-gather.5.cloned.1.call-done = bf16[1024,512]{0,1:T(8,128)(2,1)} async-done(((bf16[1024,64]{0,1:T(8,128)(2,1)}), bf16[1024,512]{0,1:T(8,128)(2,1)}) %all-gather.5.cloned.1.call-update) | async-done | bytes 1048592 | tf_op jit(solution)/shard_map/all_gather | solution.py:60
  58.2 5.9 %convolution_subtract_fusion.4 = f32[64,4096]{1,0:T(8,128)S(1)} fusion(bf16[1024,4096]{1,0:T(8,128)(2,1)} %param.6, bf16[1024,512]{0,1:T(8,128)(2,1)} %all-gather.5.cloned.1.call-done, bf16[2,64,4096]{2,1,0:T(8,128)(2,1)S(1)} %copy-done.6, s32[64]{0:T(128)S(1)} %dynamic_slice.12), kind=kOutput, calls=%fused_computation.12 | convolution fusion | flops 604602368 | bytes 11010304 | tf_op jit(solution)/shard_map/dot_general | solution.py:17
  64.1 1.7 fusion.15
  65.8 0.7 copy-done.8
  66.5 31.1 %all-reduce.6.cloned.1.call-done = f32[256,256]{1,0:T(8,128)} async-done(((f32[256,256]{1,0:T(8,128)}), f32[256,256]{1,0:T(8,128)}) %all-reduce.6.cloned.1.call-update) | async-done | bytes 262160 | tf_op jit(solution)/shard_map/psum | solution.py:76
  98.7 1.0 convolution_convert_fusion.1
  99.6 6.0 %fusion.13 = bf16[1024,64]{0,1:T(8,128)(2,1)S(1)} fusion(bf16[4096,64]{0,1:T(8,128)(2,1)S(1)} %convolution_convert_fusion.1, bf16[1024,4096]{1,0:T(8,128)(2,1)} %param.6), kind=kOutput, calls=%fused_computation.35 | convolution fusion | flops 536936448 | bytes 9043968 | tf_op jit(solution)/shard_map/dot_general | solution.py:52
  105.7 66.4 %all-reduce.8.cloned.1.call-done = f32[256,256]{1,0:T(8,128)} async-done(((f32[256,256]{1,0:T(8,128)}), f32[256,256]{1,0:T(8,128)}) %all-reduce.8.cloned.1.call-update) | async-done | bytes 262160 | tf_op jit(solution)/shard_map/psum | solution.py:77
  172.1 1.1 copy.9
  173.2 1.0 fusion.25
  174.3 11.7 %cholesky.130 = f32[128,128]{1,0:T(8,128)S(1)} custom-call(f32[128,128]{1,0:T(8,128)S(1)} %cholesky.194), custom_call_target="Cholesky" | custom-call | tf_op jit(solution)/shard_map/jit(cholesky)/cholesky | solution.py:78
  186.1 9.8 %custom-call.13 = f32[1,128,128]{1,2,0:T(8,128)S(1)} custom-call(f32[1,128,128]{2,1,0:T(8,128)S(1)} %get-tuple-element.54), custom_call_target="InvertDiagBlocksLowerTriangular" | custom-call | tf_op jit(solution)/shard_map/jit(cholesky)/cholesky | solution.py:78
  196.4 11.9 %cholesky.147 = f32[128,128]{1,0:T(8,128)S(1)} custom-call(f32[128,128]{1,0:T(8,128)S(1)} %convolution_subtract_fusion.6), custom_call_target="Cholesky" | custom-call | tf_op jit(solution)/shard_map/jit(cholesky)/cholesky | solution.py:78
  208.3 0.7 compare_reduce_fusion.3
  209.1 0.7 compare_reduce_fusion.2
  211.1 4.1 while.4
  211.2 0.6 fusion.79
  211.8 1.4 bitcast_dynamic-update-slice_fusion.4
  213.2 0.6 fusion.79
  213.9 1.4 bitcast_dynamic-update-slice_fusion.4
  215.3 19.7 %custom-call.14 = f32[2,128,128]{1,2,0:T(8,128)S(1)} custom-call(f32[2,128,128]{2,1,0:T(8,128)S(1)} %get-tuple-element.21), custom_call_target="InvertDiagBlocksLowerTriangular" | custom-call | tf_op jit(solution)/shard_map/jit(_solve_triangular)/triangular_solve | solution.py:23
  235.0 3.6 fusion.5
  238.6 1.9 convolution_subtract_fusion.1
  240.6 1.9 fusion.42
  242.5 0.8 convolution_convert_fusion.5
  243.8 0.7 pad_maximum_fusion.2
  244.7 41.0 %all-gather.9.cloned.1.call-done = bf16[1280,512]{0,1:T(8,128)(2,1)} async-done(((bf16[1280,64]{0,1:T(8,128)(2,1)}), bf16[1280,512]{0,1:T(8,128)(2,1)}) %all-gather.9.cloned.1.call-update) | async-done | bytes 1310736 | tf_op jit(solution)/shard_map/all_gather | solution.py:60
  285.7 1.7 convolution_convert_fusion.2
  287.5 5.1 %convolution_subtract_fusion.3 = f32[64,4096]{1,0:T(8,128)S(1)} fusion(bf16[1024,4096]{1,0:T(8,128)(2,1)} %param.6, bf16[2,64,4096]{2,1,0:T(8,128)(2,1)S(1)} %copy-done.7, bf16[1280,64]{0,1:T(8,128)(2,1)S(1)} %convolution_convert_fusion.2), kind=kOutput, calls=%fused_computation.11 | convolution fusion | flops 537395200 | bytes 10092544 | tf_op jit(solution)/shard_map/dot_general | solution.py:17
  293.2 1.7 fusion.16
  294.8 0.7 copy-done.9
  295.6 31.2 %all-reduce.10.cloned.1.call-done = f32[256,256]{1,0:T(8,128)} async-done(((f32[256,256]{1,0:T(8,128)}), f32[256,256]{1,0:T(8,128)}) %all-reduce.10.cloned.1.call-update) | async-done | bytes 262160 | tf_op jit(solution)/shard_map/psum | solution.py:76
  327.8 73.5 %all-reduce.12.cloned.1.call-done = f32[256,256]{1,0:T(8,128)} async-done(((f32[256,256]{1,0:T(8,128)}), f32[256,256]{1,0:T(8,128)}) %all-reduce.12.cloned.1.call-update) | async-done | bytes 262160 | tf_op jit(solution)/shard_map/psum | solution.py:77
  401.2 1.1 copy.11
  402.3 1.0 bitcast_add_fusion.1
  403.7 11.7 %cholesky.164 = f32[128,128]{1,0:T(8,128)S(1)} custom-call(f32[128,128]{1,0:T(8,128)S(1)} %cholesky.197), custom_call_target="Cholesky" | custom-call | tf_op jit(solution)/shard_map/jit(cholesky)/cholesky | solution.py:78
  415.4 9.8 %custom-call.15 = f32[1,128,128]{1,2,0:T(8,128)S(1)} custom-call(f32[1,128,128]{2,1,0:T(8,128)S(1)} %get-tuple-element.50), custom_call_target="InvertDiagBlocksLowerTriangular" | custom-call | tf_op jit(solution)/shard_map/jit(cholesky)/cholesky | solution.py:78
  425.7 11.7 %cholesky.181 = f32[128,128]{1,0:T(8,128)S(1)} custom-call(f32[128,128]{1,0:T(8,128)S(1)} %convolution_subtract_fusion.5), custom_call_target="Cholesky" | custom-call | tf_op jit(solution)/shard_map/jit(cholesky)/cholesky | solution.py:78
  440.1 4.1 while.5
  440.9 1.4 bitcast_dynamic-update-slice_fusion.5
  442.9 1.4 bitcast_dynamic-update-slice_fusion.5
  444.2 19.7 %custom-call.16 = f32[2,128,128]{1,2,0:T(8,128)S(1)} custom-call(f32[2,128,128]{2,1,0:T(8,128)S(1)} %get-tuple-element.22), custom_call_target="InvertDiagBlocksLowerTriangular" | custom-call | tf_op jit(solution)/shard_map/jit(_solve_triangular)/triangular_solve | solution.py:23
  464.0 3.6 fusion.3
  467.6 1.9 convolution_subtract_fusion
  469.6 1.9 fusion.38
  471.7 1.5 pad_maximum_fusion.1
  (80 shorter events, 8.1 us)
Async XLA Ops:
  6.5 51.7 %all-gather.5.cloned.1.call-start = ((), (), s32[]{:S(2)}) async-start(), calls=%async_computation | async-start | bytes 1179648 | tf_op jit(solution)/shard_map/all_gather | solution.py:60
  7.5 50.7 %copy-start.6 = (bf16[2,64,4096]{2,1,0:T(8,128)(2,1)S(1)}, bf16[2,64,4096]{2,1,0:T(8,128)(2,1)}, u32[]{:S(2)}) copy-start(bf16[2,64,4096]{2,1,0:T(8,128)(2,1)} %param.7) | copy-start | bytes 3145732
  15.0 82.6 %all-reduce.6.cloned.1.call-start = ((), (), s32[]{:S(2)}) async-start(), calls=%async_computation.1 | async-start | bytes 524288 | tf_op jit(solution)/shard_map/psum | solution.py:76
  64.1 33.7 %copy-start.5 = (f32[64,4096]{1,0:T(8,128)}, f32[64,4096]{1,0:T(8,128)S(1)}, u32[]{:S(2)}) copy-start(f32[64,4096]{1,0:T(8,128)S(1)} %convolution_subtract_fusion.4) | copy-start | bytes 3145732
  65.8 0.7 copy-start.8
  66.5 105.6 %all-reduce.8.cloned.1.call-start = ((), (), s32[]{:S(2)}) async-start(), calls=%async_computation.2 | async-start | bytes 524288 | tf_op jit(solution)/shard_map/psum | solution.py:77
  97.7 137.3 %all-gather.7.cloned.1.call-start = ((), (), s32[]{:S(2)}) async-start(), calls=%async_computation.3 | async-start | bytes 5242880 | tf_op jit(solution)/shard_map/all_gather | solution.py:79
  98.2 187.5 %all-gather.9.cloned.1.call-start = ((), (), s32[]{:S(2)}) async-start(), calls=%async_computation.4 | async-start | bytes 1474560 | tf_op jit(solution)/shard_map/all_gather | solution.py:60
  235.0 3.7 copy-start.2
  242.5 1.3 copy-start
  243.8 43.6 %copy-start.7 = (bf16[2,64,4096]{2,1,0:T(8,128)(2,1)S(1)}, bf16[2,64,4096]{2,1,0:T(8,128)(2,1)}, u32[]{:S(2)}) copy-start(bf16[2,64,4096]{2,1,0:T(8,128)(2,1)} %param.7) | copy-start | bytes 3145732
  244.6 82.3 %all-reduce.10.cloned.1.call-start = ((), (), s32[]{:S(2)}) async-start(), calls=%async_computation.5 | async-start | bytes 524288 | tf_op jit(solution)/shard_map/psum | solution.py:76
  287.5 5.2 %copy-start.1 = (f32[128,4096]{1,0:T(8,128)S(1)}, f32[128,4096]{1,0:T(8,128)}, u32[]{:S(2)}) copy-start(f32[128,4096]{1,0:T(8,128)} %copy-done) | copy-start | bytes 6291460
  293.1 34.2 %copy-start.4 = (f32[64,4096]{1,0:T(8,128)}, f32[64,4096]{1,0:T(8,128)S(1)}, u32[]{:S(2)}) copy-start(f32[64,4096]{1,0:T(8,128)S(1)} %convolution_subtract_fusion.2) | copy-start | bytes 3145732
  294.8 0.7 copy-start.9
  295.6 105.7 %all-reduce.12.cloned.1.call-start = ((), (), s32[]{:S(2)}) async-start(), calls=%async_computation.6 | async-start | bytes 524288 | tf_op jit(solution)/shard_map/psum | solution.py:77
  326.8 137.1 %all-gather.11.cloned.1.call-start = ((), (), s32[]{:S(2)}) async-start(), calls=%async_computation.7 | async-start | bytes 5242880 | tf_op jit(solution)/shard_map/all_gather | solution.py:79
  464.0 3.7 copy-start.3
Sparse Core Ops, SparseCore 0:
  15.2 42.9 all-gather.4
  66.6 30.9 all-reduce.5
  101.0 71.0 all-reduce.7
  173.5 33.7 all-gather.6
  244.7 41.0 all-gather.8
  295.7 31.1 all-reduce.9
  330.2 71.0 all-reduce.11
  402.8 33.7 all-gather.10
